TPU v7x, 32 devices: a whole 2x2x4 slice. The times are simulated.
32 devices in a mesh: freq: 4 (over y, x), space: 8 (over z, core).
Axes of the slice: x: 2, y: 2, z: 4, core: 2. Of those that a mesh axis runs over, the one named last changes fastest.
Arguments:
- snapshots: float32 [2, 256, 3, 4096], P(None, 'freq', None, 'space'), may hold values from -6 to 6
- mean_field: float32 [3, 4096], P(None, 'space'), may hold values from -3 to 3
- weights: float32 [3, 4096], P(None, 'space'), may hold values from 0.25 to 4
- rates: float32 [128], P('freq'), may hold values from 0.2 to 0.8
- modes: float32 [128, 2, 16, 3, 4096], P('freq', None, None, None, 'space'), may hold values from -6 to 6
Outputs:
- modes_out: float32 [128, 2, 16, 3, 4096], P('freq', None, None, None, 'space')
- coefficients: float32 [2, 128, 2, 16], P(None, 'freq')
All inputs are finite; a program needn't handle non-finite values.
Results may differ from a plain program's by a relative error of at most 0.00024.
Values sent between devices are 32-bit elements; how exact they have to be, the bound alone decides.
A program may use at most 64 MiB of HBM per device.

v0:
```python
import functools
import math

import jax
import jax.numpy as jnp
import numpy as np
from jax import lax
from jax.experimental import pallas as pl
from jax.experimental.pallas import tpu as pltpu
from jax.sharding import PartitionSpec as P

HIGHEST = lax.Precision.HIGHEST
LANES = 128


def spectral_table(length, parts):
    freqs = np.arange(length // 2)
    times = np.arange(length)
    angle = 2.0 * np.pi / length * (freqs[:, None] * times[None, :] % length)
    row = (0.5 - 0.5 * np.cos(2.0 * np.pi / length * times)) / math.sqrt(3.0 * length / 8.0)
    table = np.stack((np.cos(angle) * row, -np.sin(angle) * row))
    table = table.reshape(2, parts, -1, length).transpose(1, 0, 2, 3)
    return table.reshape(length, length).astype(np.float32)


def fold(value):
    total = value[:, :LANES]
    for start in range(LANES, value.shape[1], LANES):
        total = total + value[:, start : start + LANES]
    return total


def mul(x, y):
    return x[0] * y[0] - x[1] * y[1], x[0] * y[1] + x[1] * y[0]


def sub(x, y):
    return x[0] - y[0], x[1] - y[1]


def add(x, y):
    return x[0] + y[0], x[1] + y[1]


def conj(x):
    return x[0], -x[1]


def scale(s, x):
    return s * x[0], s * x[1]


def total(x):
    return jnp.sum(x[0], axis=0, keepdims=True), jnp.sum(x[1], axis=0, keepdims=True)


def spectra_kernel(
    nq, ns, point_count,
    snap, mean, weights, rates, table, modes_hbm,
    spec, coef, co,
    phi, recv, whole, wq, gs, gbuf, pbuf,
    phi_sem, own1_sem, own2_sem, send1, recv1, send2, recv2, send_g, recv_g, send_p, recv_p,
):
    blocks, fields, quarter, points = snap.shape
    freqs, _, _, modes_k, _ = phi.shape
    sub_points = points // nq
    groups = phi_sem.shape[0]
    per = freqs // groups
    me_q = lax.axis_index("freq")
    me_s = lax.axis_index("space")

    for g in range(groups):
        pltpu.make_async_copy(
            modes_hbm.at[pl.ds(g * per, per)], phi.at[pl.ds(g * per, per)], phi_sem.at[g]
        ).start()

    barrier = pltpu.get_barrier_semaphore()
    for d in range(1, nq):
        pl.semaphore_signal(
            barrier, inc=1, device_id={"freq": lax.rem(me_q + d, nq)},
            device_id_type=pl.DeviceIdType.MESH,
        )
    for d in range(1, ns):
        pl.semaphore_signal(
            barrier, inc=1, device_id={"space": lax.rem(me_s + d, ns)},
            device_id_type=pl.DeviceIdType.MESH,
        )
    pl.semaphore_wait(barrier, nq + ns - 2)

    def lanes_of(q):
        return pl.ds(pl.multiple_of(q * sub_points, LANES), sub_points)

    def times_of(q):
        return pl.ds(pl.multiple_of(q * quarter, 8), quarter)

    def copy1(b, d):
        to = lax.rem(me_q + d, nq)
        return pltpu.make_async_remote_copy(
            src_ref=snap.at[b, :, :, lanes_of(to)],
            dst_ref=recv.at[b, :, times_of(me_q), :],
            send_sem=send1.at[b, d], recv_sem=recv1.at[b, d],
            device_id={"freq": to}, device_id_type=pl.DeviceIdType.MESH,
        )

    def own1(b):
        return pltpu.make_async_copy(
            snap.at[b, :, :, lanes_of(me_q)], recv.at[b, :, times_of(me_q), :], own1_sem.at[b]
        )

    def copy2(b, d):
        to = lax.rem(me_q + d, nq)
        return pltpu.make_async_remote_copy(
            src_ref=whole.at[b, to],
            dst_ref=spec.at[b, :, :, lanes_of(me_q)],
            send_sem=send2.at[b, d], recv_sem=recv2.at[b, d],
            device_id={"freq": to}, device_id_type=pl.DeviceIdType.MESH,
        )

    def own2(b):
        return pltpu.make_async_copy(
            whole.at[b, me_q], spec.at[b, :, :, lanes_of(me_q)], own2_sem.at[b]
        )

    def copy_g(d):
        return pltpu.make_async_remote_copy(
            src_ref=gbuf.at[me_s], dst_ref=gbuf.at[me_s],
            send_sem=send_g.at[d], recv_sem=recv_g.at[d],
            device_id={"space": lax.rem(me_s + d, ns)}, device_id_type=pl.DeviceIdType.MESH,
        )

    def copy_p(b, d):
        return pltpu.make_async_remote_copy(
            src_ref=pbuf.at[b, me_s], dst_ref=pbuf.at[b, me_s],
            send_sem=send_p.at[b, d], recv_sem=recv_p.at[b, d],
            device_id={"space": lax.rem(me_s + d, ns)}, device_id_type=pl.DeviceIdType.MESH,
        )

    for b in range(blocks):
        for d in range(1, nq):
            copy1(b, d).start()
        own1(b).start()

    def gram(g):
        pltpu.make_async_copy(
            modes_hbm.at[pl.ds(g * per, per)], phi.at[pl.ds(g * per, per)], phi_sem.at[g]
        ).wait()
        rows = per * 2 * modes_k
        product = jnp.zeros((rows, rows), jnp.float32)
        for c in range(fields):
            left = phi[pl.ds(g * per, per), :, c].reshape(rows, points)
            product = product + lax.dot_general(
                left, left * weights[c : c + 1, :], (((1,), (1,)), ((), ())),
                precision=HIGHEST, preferred_element_type=jnp.float32,
            )
        lane = lax.broadcasted_iota(jnp.int32, (modes_k, LANES), 1)
        for f in range(per):
            start = f * 2 * modes_k
            tile = start // LANES * LANES
            block = product[start : start + 2 * modes_k, tile : tile + LANES]
            if start % LANES:
                block = pltpu.roll(block, LANES - start % LANES, 1)
            moved = pltpu.roll(block, LANES - modes_k, 1)
            real = block[:modes_k] + moved[modes_k:]
            imag = moved[:modes_k] - block[modes_k:]
            joined = jnp.where(lane < modes_k, real, pltpu.roll(imag, modes_k, 1))
            gs[pl.ds((g * per + f) * modes_k, modes_k), :] = joined

    def dft(b):
        own1(b).wait()
        for d in range(1, nq):
            copy1(b, d).wait_recv()
        for c in range(fields):
            centered = recv[b, c] - mean[c : c + 1, lanes_of(me_q)]
            rows = jnp.dot(
                table[...], centered, precision=HIGHEST, preferred_element_type=jnp.float32
            )
            whole[b, :, c] = rows.reshape(nq, 2 * freqs, sub_points)
        for d in range(1, nq):
            copy2(b, d).start()
        own2(b).start()

    def inner(b):
        own2(b).wait()
        for d in range(1, nq):
            copy2(b, d).wait_recv()
        energy = cross_r = cross_i = jnp.zeros((freqs, LANES), jnp.float32)
        for c in range(fields):
            plain = spec[b, c]
            heavy = plain * weights[c : c + 1, :]
            wq[c] = heavy
            real, imag = heavy[:freqs], heavy[freqs:]
            energy = energy + fold(real * plain[:freqs] + imag * plain[freqs:])
            if b:
                old_r, old_i = spec[b - 1, c, :freqs], spec[b - 1, c, freqs:]
                cross_r = cross_r + fold(old_r * real + old_i * imag)
                cross_i = cross_i + fold(old_r * imag - old_i * real)
        stacked = jnp.concatenate(
            [energy, cross_r, cross_i, jnp.zeros((LANES - 3 * freqs, LANES), jnp.float32)], axis=0
        )
        extra = jnp.sum(stacked.T, axis=0, keepdims=True)
        lane = lax.broadcasted_iota(jnp.int32, (modes_k, LANES), 1)

        def body(f, result):
            sum_r = jnp.zeros((modes_k, points), jnp.float32)
            sum_i = sum_r
            for c in range(fields):
                pr, pi = phi[f, 0, c], phi[f, 1, c]
                qr, qi = wq[c, pl.ds(f, 1), :], wq[c, pl.ds(freqs + f, 1), :]
                sum_r = sum_r + pr * qr + pi * qi
                sum_i = sum_i + pr * qi - pi * qr
            one_r = jnp.sum(fold(sum_r), axis=1, keepdims=True)
            one_i = jnp.sum(fold(sum_i), axis=1, keepdims=True)
            result = jnp.where(lane == f, one_r, result)
            return jnp.where(lane == freqs + f, one_i, result)

        result = lax.fori_loop(
            0, freqs, body, jnp.zeros((modes_k, LANES), jnp.float32), unroll=4
        )
        pbuf[b, me_s, pl.ds(0, modes_k), :] = result
        pbuf[b, me_s, pl.ds(modes_k, 8), :] = jnp.broadcast_to(extra, (8, LANES))
        for d in range(1, ns):
            copy_p(b, d).start()

    lax.fori_loop(0, groups // 2, lambda g, _: gram(g), None)
    dft(0)
    lax.fori_loop(groups // 2, groups, lambda g, _: gram(g), None)
    quads = gbuf.shape[1]
    each = modes_k // quads
    for m in range(quads):
        stacked = jnp.concatenate(
            [gs[pl.ds(m * each + r, freqs, stride=modes_k), :] for r in range(each)], axis=0
        )
        gbuf[me_s, m] = stacked.T[: 2 * modes_k]
    for d in range(1, ns):
        copy_g(d).start()
    for b in range(1, blocks):
        dft(b)
    for b in range(blocks):
        inner(b)

    for d in range(1, ns):
        copy_g(d).wait_recv()
    grams = gbuf[0]
    for s in range(1, ns):
        grams = grams + gbuf[s]
    gkj = []
    for j in range(modes_k):
        part = grams[j // each]
        if j % each:
            part = pltpu.roll(part, LANES - (j % each) * freqs, 1)
        gkj.append((part[:modes_k, :freqs], -part[modes_k:, :freqs]))
    diag = jnp.concatenate([gkj[k][0][k : k + 1] for k in range(modes_k)], axis=0)

    def apply_gram(x):
        out = None
        for j in range(modes_k):
            term = mul((x[0][j : j + 1], x[1][j : j + 1]), gkj[j])
            out = term if out is None else add(out, term)
        return out

    def reduced(b):
        for d in range(1, ns):
            copy_p(b, d).wait_recv()
        value = pbuf[b, 0]
        for s in range(1, ns):
            value = value + pbuf[b, s]
        head, tail = value[:modes_k], value[modes_k:]
        proj = head[:, :freqs], pltpu.roll(head, LANES - freqs, 1)[:, :freqs]
        cross = (
            pltpu.roll(tail, LANES - freqs, 1)[:1, :freqs],
            pltpu.roll(tail, LANES - 2 * freqs, 1)[:1, :freqs],
        )
        return proj, tail[:1, :freqs], cross

    shrink = 1.0 / math.sqrt(point_count)
    rate = rates[...]
    b1, qq1, _ = reduced(0)
    a1 = scale(shrink, b1)
    alpha = scale(shrink, a1)
    h1 = sub(b1, apply_gram(alpha))
    rr1 = qq1 - total(mul(alpha, conj(b1)))[0] - total(mul(conj(alpha), h1))[0]
    s1 = scale(rate / jnp.sqrt(qq1 / point_count + 1e-6), conj(a1))
    u1 = diag + 2.0 * mul(s1, h1)[0] + (s1[0] * s1[0] + s1[1] * s1[1]) * rr1
    u1 = jnp.maximum(u1, 0.0)
    id1 = 1.0 / jnp.sqrt(u1 / point_count + 1e-6)
    b2, qq2, q12 = reduced(1)
    rho = sub(q12, total(mul(conj(alpha), b2)))
    a2 = scale(id1 * shrink, add(b2, mul(conj(s1), rho)))
    c2 = scale(id1 * shrink, a2)
    e = total(mul(c2, s1))
    phi_r2 = sub(sub(b2, apply_gram(c2)), mul(e, h1))
    r1_r2 = sub(sub(rho, total(mul(c2, conj(h1)))), scale(rr1, e))
    rr2 = (
        qq2
        - total(mul(c2, conj(b2)))[0]
        - mul(e, conj(rho))[0]
        - total(mul(conj(c2), phi_r2))[0]
        - mul(conj(e), r1_r2)[0]
    )
    s2 = scale(rate / jnp.sqrt(qq2 / point_count + 1e-6), conj(a2))
    p1_r2 = scale(id1, add(phi_r2, mul(conj(s1), r1_r2)))
    u2 = id1 * id1 * u1 + 2.0 * mul(s2, p1_r2)[0] + (s2[0] * s2[0] + s2[1] * s2[1]) * rr2
    id2 = 1.0 / jnp.sqrt(jnp.maximum(u2, 0.0) / point_count + 1e-6)
    keep = id1 * id2
    first, second = scale(keep, s1), scale(id2, s2)
    for ri in range(2):
        coef[0, ri] = a1[ri]
        coef[1, ri] = a2[ri]
    wide = jnp.broadcast_to(e[0], (modes_k, freqs)), jnp.broadcast_to(e[1], (modes_k, freqs))
    for n, value in enumerate((keep, *first, *second, *alpha, *c2, *wide)):
        co[pl.ds(n * modes_k, modes_k), pl.ds(0, freqs)] = value

    for b in range(blocks):
        for d in range(1, nq):
            copy1(b, d).wait_send()
            copy2(b, d).wait_send()
        for d in range(1, ns):
            copy_p(b, d).wait_send()
    for d in range(1, ns):
        copy_g(d).wait_send()


def update_kernel(co, spec, modes, out):
    per, _, fields, modes_k, points = modes.shape
    freqs = spec.shape[2] // 2
    g = pl.program_id(0)
    table = pltpu.roll(co[...], lax.rem(LANES - g * per, LANES), 1)

    def column(n, f):
        return table[n * modes_k : (n + 1) * modes_k, f : f + 1]

    for f in range(per):
        keep, s1r, s1i, s2r, s2i, ar, ai, cr, ci, er, ei = (column(n, f) for n in range(11))
        er, ei = er[:1], ei[:1]
        row_r, row_i = pl.ds(g * per + f, 1), pl.ds(freqs + g * per + f, 1)
        for c in range(fields):
            pr, pi = modes[f, 0, c], modes[f, 1, c]
            r1r = spec[0, c, row_r, :] - jnp.sum(ar * pr - ai * pi, axis=0, keepdims=True)
            r1i = spec[0, c, row_i, :] - jnp.sum(ar * pi + ai * pr, axis=0, keepdims=True)
            r2r = spec[1, c, row_r, :] - jnp.sum(cr * pr - ci * pi, axis=0, keepdims=True)
            r2i = spec[1, c, row_i, :] - jnp.sum(cr * pi + ci * pr, axis=0, keepdims=True)
            r2r = r2r - (er * r1r - ei * r1i)
            r2i = r2i - (er * r1i + ei * r1r)
            out[f, 0, c] = keep * pr + (s1r * r1r - s1i * r1i) + (s2r * r2r - s2i * r2i)
            out[f, 1, c] = keep * pi + (s1r * r1i + s1i * r1r) + (s2r * r2i + s2i * r2r)


def per_device(snapshots, mean_field, weights, rates, modes):
    nq, ns = lax.axis_size("freq"), lax.axis_size("space")
    blocks, quarter, fields, points = snapshots.shape
    freqs, _, modes_k = modes.shape[:3]
    length = quarter * nq
    sub_points = points // nq
    point_count = fields * points * ns
    snap = snapshots.transpose(0, 2, 1, 3)
    field = modes.transpose(0, 1, 3, 2, 4)
    per = LANES * 2 // (2 * modes_k)
    groups = freqs // per
    quads = modes_k * freqs // LANES
    vmem = pl.BlockSpec(memory_space=pltpu.VMEM)
    dma = pltpu.SemaphoreType.DMA
    f32 = jnp.float32
    spec, coef, co = pl.pallas_call(
        functools.partial(spectra_kernel, nq, ns, point_count),
        out_shape=(
            jax.ShapeDtypeStruct((blocks, fields, 2 * freqs, points), f32),
            jax.ShapeDtypeStruct((blocks, 2, modes_k, freqs), f32),
            jax.ShapeDtypeStruct((11 * modes_k, LANES), f32),
        ),
        in_specs=[vmem] * 5 + [pl.BlockSpec(memory_space=pl.ANY)],
        out_specs=(vmem, vmem, vmem),
        scratch_shapes=[
            pltpu.VMEM((freqs, 2, fields, modes_k, points), f32),
            pltpu.VMEM((blocks, fields, length, sub_points), f32),
            pltpu.VMEM((blocks, nq, fields, 2 * freqs, sub_points), f32),
            pltpu.VMEM((fields, 2 * freqs, points), f32),
            pltpu.VMEM((freqs * modes_k, LANES), f32),
            pltpu.VMEM((ns, quads, 2 * modes_k, LANES), f32),
            pltpu.VMEM((blocks, ns, modes_k + 8, LANES), f32),
            dma((groups,)),
            dma((blocks,)),
            dma((blocks,)),
            dma((blocks, nq)),
            dma((blocks, nq)),
            dma((blocks, nq)),
            dma((blocks, nq)),
            dma((ns,)),
            dma((ns,)),
            dma((blocks, ns)),
            dma((blocks, ns)),
        ],
        compiler_params=pltpu.CompilerParams(collective_id=0, has_side_effects=True),
        name="spectra",
    )(
        snap, mean_field, weights, rates.reshape(1, freqs),
        jnp.asarray(spectral_table(length, nq)), field,
    )
    step = 4
    block = (step, 2, fields, modes_k, points)
    updated = pl.pallas_call(
        update_kernel,
        grid=(freqs // step,),
        out_shape=jax.ShapeDtypeStruct(field.shape, f32),
        in_specs=[vmem, vmem, pl.BlockSpec(block, lambda g: (g, 0, 0, 0, 0))],
        out_specs=pl.BlockSpec(block, lambda g: (g, 0, 0, 0, 0)),
        compiler_params=pltpu.CompilerParams(dimension_semantics=("arbitrary",)),
        name="update",
    )(co, spec, field)
    return updated.transpose(0, 1, 3, 2, 4), coef.transpose(0, 3, 1, 2)


def solution(mesh):
    return jax.shard_map(
        per_device,
        mesh=mesh,
        in_specs=(
            P(None, "freq", None, "space"),
            P(None, "space"),
            P(None, "space"),
            P("freq"),
            P("freq", None, None, None, "space"),
        ),
        out_specs=(P("freq", None, None, None, "space"), P(None, "freq", None, None)),
        check_vma=False,
    )
```

profile of v0, /device:TPU:0, one launch (start us, length us, event | category | flops | bytes accessed | tf_op | source)
XLA Modules:
  0.0 48.5 jit_solution(18148289477995461268)
XLA Ops:
  0.6 35.6 %spectra.1 = (f32[2,3,64,512]{3,2,1,0:T(8,128)}, f32[2,2,16,32]{3,2,1,0:T(8,128)}, f32[176,128]{1,0:T(8,128)}) custom-call(f32[2,3,64,512]{3,2,1,0:T(8,128)} %bitcast.8, f32[3,512]{1,0:T(4,128)} %mean.1, f32[3,512]{1,0:T(4,128)} %weights.1, f32[1,32]{1,0:T(1,128)} %bitcast.10, f32[256,256]{1,0:T(8,128)} %constant.2.clone.table, f32[32,2,3,16,512]{4,3,2,1,0:T(8,128)} %bitcast.5), custom_call_target="tpu_custom_call" | custom-call | tf_op jit(solution)/shard_map/spectra/pallas_call | solution.py:363
  36.2 0.0 copy-start
  36.2 11.6 %update.1 = f32[32,2,3,16,512]{4,3,2,1,0:T(8,128)} custom-call(f32[176,128]{1,0:T(8,128)} %get-tuple-element.5.co, f32[2,3,64,512]{3,2,1,0:T(8,128)} %get-tuple-element.6.spec, f32[32,2,3,16,512]{4,3,2,1,0:T(8,128)} %bitcast.6), custom_call_target="tpu_custom_call" | custom-call | tf_op jit(solution)/shard_map/update/pallas_call | solution.py:400
  47.8 0.0 copy-done
  47.9 0.6 %copy.9 = f32[2,32,2,16]{1,3,2,0:T(8,128)} copy(f32[2,32,2,16]{1,3,2,0:T(8,128)S(1)} %bitcast.9) | data formatting | bytes 16384
Async XLA Ops:
  36.2 11.6 %copy-start = (f32[2,2,16,32]{3,2,1,0:T(8,128)S(1)}, f32[2,2,16,32]{3,2,1,0:T(8,128)}, u32[]{:S(2)}) copy-start(f32[2,2,16,32]{3,2,1,0:T(8,128)} %get-tuple-element.7) | copy-start | bytes 24580
where the time goes:
time: 48.8 us; the launch traced here: 48.5 us
  Pallas kernels  47.2 us (97%)
  between operations  0.65 us (1%)
  local copies, waits for them, and re-layouts  0.62 us (1%)
    pallas_call x1, Pallas kernels, per_device(): pl.pallas_call(functools.partial(spectra_kernel, nq, ns, point_count), ou...  35.6 us
    pallas_call x1, Pallas kernels, per_device(): pl.pallas_call(update_kernel, grid=(freqs // step,), out_shape=jax.ShapeD...  11.6 us

commit v1 on v0

--- a/solution.py
+++ b/solution.py
@@ -30,6 +30,15 @@
     return total
 
 
+def split_dot(x, y, axis):
+    dims = (((1,), (axis,)), ((), ()))
+    xh, yh = x.astype(jnp.bfloat16), y.astype(jnp.bfloat16)
+    xl = (x - xh.astype(jnp.float32)).astype(jnp.bfloat16)
+    yl = (y - yh.astype(jnp.float32)).astype(jnp.bfloat16)
+    dot = functools.partial(lax.dot_general, dimension_numbers=dims, preferred_element_type=jnp.float32)
+    return dot(xh, yh) + (dot(xh, yl) + dot(xl, yh))
+
+
 def mul(x, y):
     return x[0] * y[0] - x[1] * y[1], x[0] * y[1] + x[1] * y[0]
 
@@ -58,8 +67,8 @@
     nq, ns, point_count,
     snap, mean, weights, rates, table, modes_hbm,
     spec, coef, co,
-    phi, recv, whole, wq, gs, gbuf, pbuf,
-    phi_sem, own1_sem, own2_sem, send1, recv1, send2, recv2, send_g, recv_g, send_p, recv_p,
+    phi, recv, whole, wq, gs, gsend, grecv, gbuf, pbuf,
+    phi_sem, own1_sem, own2_sem, send1, recv1, send2, recv2, send_r, recv_r, send_g, recv_g, send_p, recv_p,
 ):
     blocks, fields, quarter, points = snap.shape
     freqs, _, _, modes_k, _ = phi.shape
@@ -121,6 +130,14 @@
             whole.at[b, me_q], spec.at[b, :, :, lanes_of(me_q)], own2_sem.at[b]
         )
 
+    def copy_r(d):
+        to = lax.rem(me_s + d, ns)
+        return pltpu.make_async_remote_copy(
+            src_ref=gsend.at[to], dst_ref=grecv.at[me_s],
+            send_sem=send_r.at[d], recv_sem=recv_r.at[d],
+            device_id={"space": to}, device_id_type=pl.DeviceIdType.MESH,
+        )
+
     def copy_g(d):
         return pltpu.make_async_remote_copy(
             src_ref=gbuf.at[me_s], dst_ref=gbuf.at[me_s],
@@ -148,10 +165,7 @@
         product = jnp.zeros((rows, rows), jnp.float32)
         for c in range(fields):
             left = phi[pl.ds(g * per, per), :, c].reshape(rows, points)
-            product = product + lax.dot_general(
-                left, left * weights[c : c + 1, :], (((1,), (1,)), ((), ())),
-                precision=HIGHEST, preferred_element_type=jnp.float32,
-            )
+            product = product + split_dot(left, left * weights[c : c + 1, :], 1)
         lane = lax.broadcasted_iota(jnp.int32, (modes_k, LANES), 1)
         for f in range(per):
             start = f * 2 * modes_k
@@ -171,9 +185,7 @@
             copy1(b, d).wait_recv()
         for c in range(fields):
             centered = recv[b, c] - mean[c : c + 1, lanes_of(me_q)]
-            rows = jnp.dot(
-                table[...], centered, precision=HIGHEST, preferred_element_type=jnp.float32
-            )
+            rows = split_dot(table[...], centered, 0)
             whole[b, :, c] = rows.reshape(nq, 2 * freqs, sub_points)
         for d in range(1, nq):
             copy2(b, d).start()
@@ -198,51 +210,70 @@
             [energy, cross_r, cross_i, jnp.zeros((LANES - 3 * freqs, LANES), jnp.float32)], axis=0
         )
         extra = jnp.sum(stacked.T, axis=0, keepdims=True)
+        wide = jnp.broadcast_to(extra, (modes_k, LANES))
         lane = lax.broadcasted_iota(jnp.int32, (modes_k, LANES), 1)
 
         def body(f, result):
-            sum_r = jnp.zeros((modes_k, points), jnp.float32)
+            sum_r = jnp.zeros((modes_k, LANES), jnp.float32)
             sum_i = sum_r
             for c in range(fields):
-                pr, pi = phi[f, 0, c], phi[f, 1, c]
-                qr, qi = wq[c, pl.ds(f, 1), :], wq[c, pl.ds(freqs + f, 1), :]
-                sum_r = sum_r + pr * qr + pi * qi
-                sum_i = sum_i + pr * qi - pi * qr
-            one_r = jnp.sum(fold(sum_r), axis=1, keepdims=True)
-            one_i = jnp.sum(fold(sum_i), axis=1, keepdims=True)
+                row_r, row_i = wq[c, pl.ds(f, 1), :], wq[c, pl.ds(freqs + f, 1), :]
+                for start in range(0, points, LANES):
+                    tile = slice(start, start + LANES)
+                    pr, pi = phi[f, 0, c, :, tile], phi[f, 1, c, :, tile]
+                    qr, qi = row_r[:, tile], row_i[:, tile]
+                    sum_r = sum_r + (pr * qr + pi * qi)
+                    sum_i = sum_i + (pr * qi - pi * qr)
+            one_r = jnp.sum(sum_r, axis=1, keepdims=True)
+            one_i = jnp.sum(sum_i, axis=1, keepdims=True)
             result = jnp.where(lane == f, one_r, result)
             return jnp.where(lane == freqs + f, one_i, result)
 
         result = lax.fori_loop(
             0, freqs, body, jnp.zeros((modes_k, LANES), jnp.float32), unroll=4
         )
-        pbuf[b, me_s, pl.ds(0, modes_k), :] = result
-        pbuf[b, me_s, pl.ds(modes_k, 8), :] = jnp.broadcast_to(extra, (8, LANES))
+        row = lax.broadcasted_iota(jnp.int32, (modes_k, LANES), 0)
+        side = jnp.where(
+            row == 0, pltpu.roll(wide, 2 * freqs, 1),
+            jnp.where(row == 1, pltpu.roll(wide, freqs, 1), wide),
+        )
+        pbuf[b, me_s] = jnp.where(lane < 2 * freqs, result, side)
         for d in range(1, ns):
             copy_p(b, d).start()
 
     lax.fori_loop(0, groups // 2, lambda g, _: gram(g), None)
     dft(0)
     lax.fori_loop(groups // 2, groups, lambda g, _: gram(g), None)
-    quads = gbuf.shape[1]
-    each = modes_k // quads
+    each = LANES // freqs
+    quads = modes_k // each
+    piece = gsend.shape[1]
+    owners = 2 * modes_k // piece
     for m in range(quads):
         stacked = jnp.concatenate(
             [gs[pl.ds(m * each + r, freqs, stride=modes_k), :] for r in range(each)], axis=0
         )
-        gbuf[me_s, m] = stacked.T[: 2 * modes_k]
-    for d in range(1, ns):
-        copy_g(d).start()
+        turned = stacked.T
+        for o in range(owners):
+            gsend[m * owners + o] = turned[o * piece : (o + 1) * piece]
+    for d in range(1, ns):
+        copy_r(d).start()
+    grecv[me_s] = gsend[me_s]
     for b in range(1, blocks):
         dft(b)
+    for d in range(1, ns):
+        copy_r(d).wait_recv()
+    own = grecv[0]
+    for s in range(1, ns):
+        own = own + grecv[s]
+    gbuf[me_s] = own
+    for d in range(1, ns):
+        copy_g(d).start()
     for b in range(blocks):
         inner(b)
 
     for d in range(1, ns):
         copy_g(d).wait_recv()
-    grams = gbuf[0]
-    for s in range(1, ns):
-        grams = grams + gbuf[s]
+    grams = gbuf[...].reshape(quads, 2 * modes_k, LANES)
     gkj = []
     for j in range(modes_k):
         part = grams[j // each]
@@ -264,13 +295,9 @@
         value = pbuf[b, 0]
         for s in range(1, ns):
             value = value + pbuf[b, s]
-        head, tail = value[:modes_k], value[modes_k:]
-        proj = head[:, :freqs], pltpu.roll(head, LANES - freqs, 1)[:, :freqs]
-        cross = (
-            pltpu.roll(tail, LANES - freqs, 1)[:1, :freqs],
-            pltpu.roll(tail, LANES - 2 * freqs, 1)[:1, :freqs],
-        )
-        return proj, tail[:1, :freqs], cross
+        side = pltpu.roll(value, LANES - 2 * freqs, 1)[:, :freqs]
+        proj = value[:, :freqs], pltpu.roll(value, LANES - freqs, 1)[:, :freqs]
+        return proj, side[:1], (side[1:2], side[2:3])
 
     shrink = 1.0 / math.sqrt(point_count)
     rate = rates[...]
@@ -317,6 +344,7 @@
         for d in range(1, ns):
             copy_p(b, d).wait_send()
     for d in range(1, ns):
+        copy_r(d).wait_send()
         copy_g(d).wait_send()
 
 
@@ -330,19 +358,26 @@
         return table[n * modes_k : (n + 1) * modes_k, f : f + 1]
 
     for f in range(per):
-        keep, s1r, s1i, s2r, s2i, ar, ai, cr, ci, er, ei = (column(n, f) for n in range(11))
+        keep, s1r, s1i, s2r, s2i, ar, ai, cr, ci, er, ei = (
+            jnp.broadcast_to(column(n, f), (modes_k, LANES)) for n in range(11)
+        )
         er, ei = er[:1], ei[:1]
         row_r, row_i = pl.ds(g * per + f, 1), pl.ds(freqs + g * per + f, 1)
         for c in range(fields):
-            pr, pi = modes[f, 0, c], modes[f, 1, c]
-            r1r = spec[0, c, row_r, :] - jnp.sum(ar * pr - ai * pi, axis=0, keepdims=True)
-            r1i = spec[0, c, row_i, :] - jnp.sum(ar * pi + ai * pr, axis=0, keepdims=True)
-            r2r = spec[1, c, row_r, :] - jnp.sum(cr * pr - ci * pi, axis=0, keepdims=True)
-            r2i = spec[1, c, row_i, :] - jnp.sum(cr * pi + ci * pr, axis=0, keepdims=True)
-            r2r = r2r - (er * r1r - ei * r1i)
-            r2i = r2i - (er * r1i + ei * r1r)
-            out[f, 0, c] = keep * pr + (s1r * r1r - s1i * r1i) + (s2r * r2r - s2i * r2i)
-            out[f, 1, c] = keep * pi + (s1r * r1i + s1i * r1r) + (s2r * r2i + s2i * r2r)
+            q1r, q1i, q2r, q2i = (spec[b, c, row, :] for b in range(2) for row in (row_r, row_i))
+            for start in range(0, points, LANES):
+                tile = slice(start, start + LANES)
+                pr, pi = modes[f, 0, c, :, tile], modes[f, 1, c, :, tile]
+                r1r = q1r[:, tile] - jnp.sum(ar * pr - ai * pi, axis=0, keepdims=True)
+                r1i = q1i[:, tile] - jnp.sum(ar * pi + ai * pr, axis=0, keepdims=True)
+                r2r = q2r[:, tile] - jnp.sum(cr * pr - ci * pi, axis=0, keepdims=True)
+                r2i = q2i[:, tile] - jnp.sum(cr * pi + ci * pr, axis=0, keepdims=True)
+                r2r = r2r - (er * r1r - ei * r1i)
+                r2i = r2i - (er * r1i + ei * r1r)
+                real = keep * pr + (s1r * r1r - s1i * r1i) + (s2r * r2r - s2i * r2i)
+                imag = keep * pi + (s1r * r1i + s1i * r1r) + (s2r * r2i + s2i * r2r)
+                out[f, 0, c, :, tile] = real
+                out[f, 1, c, :, tile] = imag
 
 
 def per_device(snapshots, mean_field, weights, rates, modes):
@@ -356,7 +391,7 @@
     field = modes.transpose(0, 1, 3, 2, 4)
     per = LANES * 2 // (2 * modes_k)
     groups = freqs // per
-    quads = modes_k * freqs // LANES
+    piece = 2 * modes_k * modes_k * freqs // LANES // ns
     vmem = pl.BlockSpec(memory_space=pltpu.VMEM)
     dma = pltpu.SemaphoreType.DMA
     f32 = jnp.float32
@@ -375,8 +410,10 @@
             pltpu.VMEM((blocks, nq, fields, 2 * freqs, sub_points), f32),
             pltpu.VMEM((fields, 2 * freqs, points), f32),
             pltpu.VMEM((freqs * modes_k, LANES), f32),
-            pltpu.VMEM((ns, quads, 2 * modes_k, LANES), f32),
-            pltpu.VMEM((blocks, ns, modes_k + 8, LANES), f32),
+            pltpu.VMEM((ns, piece, LANES), f32),
+            pltpu.VMEM((ns, piece, LANES), f32),
+            pltpu.VMEM((ns, piece, LANES), f32),
+            pltpu.VMEM((blocks, ns, modes_k, LANES), f32),
             dma((groups,)),
             dma((blocks,)),
             dma((blocks,)),
@@ -384,6 +421,8 @@
             dma((blocks, nq)),
             dma((blocks, nq)),
             dma((blocks, nq)),
+            dma((ns,)),
+            dma((ns,)),
             dma((ns,)),
             dma((ns,)),
             dma((blocks, ns)),
@@ -395,7 +434,7 @@
         snap, mean_field, weights, rates.reshape(1, freqs),
         jnp.asarray(spectral_table(length, nq)), field,
     )
-    step = 4
+    step = 8
     block = (step, 2, fields, modes_k, points)
     updated = pl.pallas_call(
         update_kernel,

time: 48.8 us -> 43.5 us (0.89)
  Pallas kernels: 47.2 us -> 42 us
    pallas_call x1, Pallas kernels: 35.6 us -> 32.1 us  [per_device(): pl.pallas_call(functools.partial(spectra_kernel, nq, ns, point_count), ou...]
    pallas_call x1, Pallas kernels: 11.6 us -> 9.85 us  [per_device(): pl.pallas_call(update_kernel, grid=(freqs // step,), out_shape=jax.ShapeD...]
where the time goes in v1:
time: 43.5 us; the launch traced here: 43.2 us
  Pallas kernels  42 us (97%)
  between operations  0.65 us (1%)
  local copies, waits for them, and re-layouts  0.62 us (1%)
    pallas_call x1, Pallas kernels, per_device(): pl.pallas_call(functools.partial(spectra_kernel, nq, ns, point_count), ou...  32.1 us
    pallas_call x1, Pallas kernels, per_device(): pl.pallas_call(update_kernel, grid=(freqs // step,), out_shape=jax.ShapeD...  9.85 us

profile of v1, /device:TPU:0, one launch (start us, length us, event | category | flops | bytes accessed | tf_op | source)
XLA Modules:
  0.0 43.2 jit_solution(17343870639421071069)
XLA Ops:
  0.6 32.1 %spectra.1 = (f32[2,3,64,512]{3,2,1,0:T(8,128)}, f32[2,2,16,32]{3,2,1,0:T(8,128)}, f32[176,128]{1,0:T(8,128)}) custom-call(f32[2,3,64,512]{3,2,1,0:T(8,128)} %bitcast.8, f32[3,512]{1,0:T(4,128)} %mean.1, f32[3,512]{1,0:T(4,128)} %weights.1, f32[1,32]{1,0:T(1,128)} %bitcast.10, f32[256,256]{1,0:T(8,128)} %constant.2.clone.table, f32[32,2,3,16,512]{4,3,2,1,0:T(8,128)} %bitcast.5), custom_call_target="tpu_custom_call" | custom-call | tf_op jit(solution)/shard_map/spectra/pallas_call | solution.py:398
  32.8 0.0 copy-start
  32.8 9.8 %update.1 = f32[32,2,3,16,512]{4,3,2,1,0:T(8,128)} custom-call(f32[176,128]{1,0:T(8,128)} %get-tuple-element.5.co, f32[2,3,64,512]{3,2,1,0:T(8,128)} %get-tuple-element.6.spec, f32[32,2,3,16,512]{4,3,2,1,0:T(8,128)} %bitcast.6), custom_call_target="tpu_custom_call" | custom-call | tf_op jit(solution)/shard_map/update/pallas_call | solution.py:439
  42.6 0.0 copy-done
  42.6 0.6 %copy.9 = f32[2,32,2,16]{1,3,2,0:T(8,128)} copy(f32[2,32,2,16]{1,3,2,0:T(8,128)S(1)} %bitcast.9) | data formatting | bytes 16384
Async XLA Ops:
  32.8 9.9 %copy-start = (f32[2,2,16,32]{3,2,1,0:T(8,128)S(1)}, f32[2,2,16,32]{3,2,1,0:T(8,128)}, u32[]{:S(2)}) copy-start(f32[2,2,16,32]{3,2,1,0:T(8,128)} %get-tuple-element.7) | copy-start | bytes 24580
